TPU v7x, 512 devices: a whole 4x8x8 slice. The times are simulated.
512 devices in a mesh: blk: 32 (over x_lo, y, core), col: 16 (over x_hi, z).
Axes of the slice: x: 4 (x_hi: 2, x_lo: 2; x = x_hi * 2 + x_lo), y: 8, z: 8, core: 2. Of those that a mesh axis runs over, the one named last changes fastest.
Arguments:
- documents: bfloat16 [24576, 768], P('blk'), may hold values from -6 to 6
- landmarks: bfloat16 [65536, 768], P(('blk', 'col')), may hold values from -6 to 6
- eigen_vectors: bfloat16 [65536, 256], P(('blk', 'col')), may hold values from -6 to 6
- land_degree: float32 [65536], P(('blk', 'col')), may hold values from 0.5 to 8
- eigen_values: float32 [256], replicated, may hold values from 0.005 to 0.05
- tile_mask: int32 [192, 512], P('blk'), may hold values from 0 to 1, as said below
- labels: int32 [24576], P(('blk', 'col')), may hold values from 0 to 999
Outputs:
- embedding: float32 [24576, 256], P(('blk', 'col'))
- centroids: float32 [1000, 256], replicated
Inputs may be any that keep to these rules, and one draw needn't show every extreme that they name: `tile_mask`: 1 marks a live tile of 128 documents by 128 landmarks; every document block has at least one live tile.
All inputs are finite; a program needn't handle non-finite values.
Results may differ from a plain program's by a relative error of at most 0.0041.
Values may be sent and summed in bfloat16 or wider, within the bound.
A program may use at most 64 MiB of HBM per device.

v0:
```python
import jax
import jax.numpy as jnp
from jax import lax
from jax.sharding import PartitionSpec as P

C = 1000
BLOCK = 128


def side_by_side(arrays, axis, dim, along):
    ends, at = ([], 0)
    for a in arrays[:-1]:
        at += a.shape[along]
        ends.append(at)
    both = jnp.concatenate(arrays, axis=along)
    return tuple(jnp.split(lax.all_gather(both, axis, axis=dim, tiled=True), ends, axis=along))


def split_up(value, dim, peers):
    shape = value.shape
    parts = value.reshape(*shape[:dim], peers, shape[dim] // peers, *shape[dim + 1 :])
    return jnp.moveaxis(parts, dim, 0)


def sent_and_summed(value, axis, dim):
    peers = lax.axis_size(axis)
    parts = lax.all_to_all(split_up(value, dim, peers), axis, 0, 0, tiled=True)
    return jnp.sum(parts, axis=0)


def in_one_piece(arrays, axis, dim, along):
    columns = [a.reshape(*a.shape[:along], -1) for a in arrays]
    both = jnp.concatenate(columns, axis=along)
    whole, at, outs = (sent_and_summed(both, axis, dim), 0, [])
    for a, column in zip(arrays, columns):
        share = whole[..., at : at + column.shape[along]]
        outs.append(share.reshape(*share.shape[:along], *a.shape[along:]))
        at += column.shape[along]
    return tuple(outs)


def body(documents, landmarks, eigen_vectors, land_degree, eigen_values, tile_mask, labels):
    inverse_width = 4.0 / documents.shape[1]
    land_rows = landmarks.shape[0]
    doc_rows = documents.shape[0]
    col_index = lax.axis_index("col")
    col_count = lax.axis_size("col")
    scaled = (
        eigen_vectors.astype(jnp.float32) * lax.rsqrt(land_degree)[:, None] / eigen_values[None, :]
    ).astype(jnp.bfloat16)
    doc_square = jnp.sum(jnp.square(documents.astype(jnp.float32)), 1)
    initial = (
        jnp.zeros((doc_rows, scaled.shape[1]), jnp.float32),
        jnp.zeros((doc_rows,), jnp.float32),
    )
    land_piece, vector_piece = side_by_side((landmarks, scaled), "blk", 0, 1)
    piece_rows = land_piece.shape[0]
    offsets = jnp.arange(piece_rows, dtype=jnp.int32)
    whole_rows = (
        offsets // land_rows * (land_rows * col_count) + col_index * land_rows + offsets % land_rows
    )
    live_cols = jnp.take(tile_mask, whole_rows // BLOCK, axis=1)

    def compute(state):
        land_square = jnp.sum(jnp.square(land_piece.astype(jnp.float32)), 1)
        products = jnp.einsum(
            "df,lf->dl", documents, land_piece, preferred_element_type=jnp.float32
        )
        keep = jnp.repeat(live_cols, BLOCK, axis=0).astype(jnp.float32)
        weights = (
            jnp.exp(inverse_width * (2.0 * products - doc_square[:, None] - land_square[None, :]))
            * keep
        )
        total = jnp.dot(
            weights.astype(jnp.bfloat16), vector_piece, preferred_element_type=jnp.float32
        )
        return (total, jnp.sum(weights, 1))

    projection, degree = lax.cond(jnp.any(live_cols > 0), compute, lambda state: state, initial)
    projection, degree = in_one_piece((projection, degree), "col", 0, 1)
    embedding = projection * lax.rsqrt(degree)[:, None]
    unit_rows = embedding * lax.rsqrt(jnp.sum(jnp.square(embedding), 1, keepdims=True) + 1e-06)
    one_hot = (jnp.arange(C, dtype=jnp.int32)[:, None] == labels[None, :]).astype(jnp.float32)
    partial_sums = jnp.dot(
        one_hot, unit_rows, precision=lax.Precision.HIGHEST, preferred_element_type=jnp.float32
    )
    centroids = lax.psum(partial_sums, ("blk", "col"))
    return (embedding, centroids)


def solution(mesh):
    placed = (
        P("blk", None),
        P(("blk", "col"), None),
        P(("blk", "col"), None),
        P(("blk", "col")),
        P(),
        P("blk", None),
        P(("blk", "col")),
    )
    return jax.shard_map(
        body, mesh=mesh, in_specs=placed, out_specs=(P(("blk", "col"), None), P()), check_vma=False
    )
```

profile of v0, /device:TPU:1, one launch (start us, length us, event | category | flops | bytes accessed | tf_op | source)
XLA Modules:
  0.0 429.7 jit_solution(15334240320638322248)
XLA Ops:
  7.2 0.0 copy-start.1
  7.2 0.0 all-gather.2.cloned.1.call-start
  7.2 0.7 rsqrt.15
  8.0 0.9 divide_convert_fusion
  8.9 1.7 pad_maximum_fusion.1
  10.6 0.0 all-gather.2.cloned.1.call-update
  10.6 0.0 all-reduce.2.cloned.1.call-start
  10.6 0.9 copy.11
  11.5 0.1 compare_select_fusion
  11.6 10.8 %gather_fusion = s32[4096,6]{1,0:T(8,128)S(1)} fusion(s32[6,512]{0,1:T(8,128)S(1)} %copy.11, s32[4096]{0:T(1024)S(1)} %broadcast_clamp_fusion), kind=kCustom, calls=%fused_computation | custom fusion | bytes 212992 | tf_op jit(solution)/shard_map/jit(_take)/gather | solution.py:62
  22.5 3.8 compare_reduce_fusion
  26.9 0.0 copy-done.1
  27.0 0.2 convert_element_type.29
  27.1 63.7 %all-gather.2.cloned.1.call-done = bf16[4096,1024]{1,0:T(8,128)(2,1)} async-done(((bf16[128,1024]{1,0:T(8,128)(2,1)}), bf16[4096,1024]{1,0:T(8,128)(2,1)}) %all-gather.2.cloned.1.call-update) | async-done | bytes 8388624 | tf_op jit(solution)/shard_map/all_gather | solution.py:16
  90.8 17.6 %conditional.1 = (f32[16,48,256]{2,1,0:T(8,128)S(1)}, f32[16,48,1]{2,1,0:T(8,128)S(1)}) conditional(s32[]{:T(128)} %convert_element_type.26, () %tuple.20, (bf16[4096,1024]{1,0:T(8,128)(2,1)}, bf16[768,768]{1,0:T(8,128)(2,1)S(1)}, f32[768,768]{1,0:T(8,128)S(1)}, s32[6,4096]{0,1:T(8,128)}) %tuple.37), branch_computations={%region_1.2_spmd, %region_2.6_spmd} | conditional | flops 6475106304 | bytes 65716268 | solution.py:79
  90.8 2.9 copy.12
  93.7 1.1 convert_element_type.19
  94.8 0.2 multiply_reduce_fusion.1
  95.0 4.4 %multiply_reduce_fusion = f32[4096]{0:T(1024)S(1)} fusion(bf16[4096,1024]{1,0:T(8,128)(2,1)} %get-tuple-element.17), kind=kLoop, calls=%fused_computation.2 | loop fusion | flops 9433088 | bytes 6307840 | tf_op jit(solution)/shard_map/cond/branch_1_fun/reduce_sum | solution.py:65
  99.4 6.9 %fusion = (f32[768]{0:T(1024)S(1)}, bf16[768,4096]{1,0:T(8,128)(2,1)S(1)}) fusion(f32[6,4096]{1,0:T(8,128)S(1)} %convert_element_type.19, f32[4096]{0:T(1024)S(1)} %multiply_reduce_fusion, f32[768]{0:T(1024)S(1)} %multiply_reduce_fusion.1, bf16[768,768]{1,0:T(8,128)(2,1)S(1)} %get-tuple-element.16, bf16[4096,1024]{1,0:T(8,128)(2,1)S(1)} %copy-done), kind=kOutput, calls=%fused_computation.3 | convolution fusion | flops 4853857280 | bytes 13917184 | tf_op jit(solution)/shard_map/cond/branch_1_fun/df,lf->dl/dot_general | solution.py:66
  106.3 1.8 fusion.4
  108.1 0.3 concatenate.17
  108.4 0.1 pad_maximum_fusion
  108.5 39.7 %all_to_all.5 = f32[16,48,257]{2,1,0:T(8,128)S(1)} all-to-all(f32[16,48,257]{2,1,0:T(8,128)S(1)} %pad_maximum_fusion), channel_id=1, replica_groups=mesh['blk'=32,'col'=16] {'col'}, dimensions={0} | all-to-all | bytes 1579008 | tf_op jit(solution)/shard_map/all_to_all | solution.py:27
  148.2 0.1 reduce_sum.46
  148.2 0.1 fusion.13
  148.4 0.2 multiply_reduce_fusion.2
  148.5 0.0 copy-start.2
  148.6 1.6 fusion.6
  150.2 0.0 all-reduce.2.cloned.1.call-update
  150.2 270.4 %all-reduce.2.cloned.1.call-done = f32[1000,256]{1,0:T(8,128)} async-done(((f32[1000,256]{1,0:T(8,128)}), f32[1000,256]{1,0:T(8,128)}) %all-reduce.2.cloned.1.call-update) | async-done | bytes 1024016 | tf_op jit(solution)/shard_map/psum | solution.py:87
  420.6 2.2 copy.21
  (8 shorter events, 0.0 us)
Async XLA Ops:
  7.2 19.8 %copy-start.1 = (bf16[768,768]{1,0:T(8,128)(2,1)S(1)}, bf16[768,768]{1,0:T(8,128)(2,1)}, u32[]{:S(2)}) copy-start(bf16[768,768]{1,0:T(8,128)(2,1)} %param.9) | copy-start | bytes 3538948
  7.2 83.6 %all-gather.2.cloned.1.call-start = ((), (), s32[]{:S(2)}) async-start(), calls=%async_computation.1 | async-start | bytes 8650752 | tf_op jit(solution)/shard_map/all_gather | solution.py:16
  10.6 410.0 %all-reduce.2.cloned.1.call-start = ((), (), s32[]{:S(2)}) async-start(), calls=%async_computation.2 | async-start | bytes 2048000 | tf_op jit(solution)/shard_map/psum | solution.py:87
  90.8 57.8 %copy-start.3 = (s32[48]{0:T(128)S(1)}, s32[48]{0:T(128)}, u32[]{:S(2)}) copy-start(s32[48]{0:T(128)} %param.15) | copy-start | bytes 580
  93.7 5.7 %copy-start = (bf16[4096,1024]{1,0:T(8,128)(2,1)S(1)}, bf16[4096,1024]{1,0:T(8,128)(2,1)}, u32[]{:S(2)}) copy-start(bf16[4096,1024]{1,0:T(8,128)(2,1)} %get-tuple-element.17) | copy-start | bytes 25165828 | tf_op jit(solution)/shard_map/cond
  148.5 274.3 %copy-start.2 = (f32[48,256]{1,0:T(8,128)}, f32[48,256]{1,0:T(8,128)S(1)}, u32[]{:S(2)}) copy-start(f32[48,256]{1,0:T(8,128)S(1)} %get-tuple-element.45) | copy-start | bytes 147460
Sparse Core Ops, SparseCore 0:
  10.7 80.0 all-gather.1
  150.3 270.2 all-reduce.1
where the time goes:
time: 430 us
  waiting for transfers between devices  334 us (78%)
  blocking collectives  39.7 us (9%)
  local copies, waits for them, and re-layouts  17.9 us (4%)
  between operations  14.8 us (3%)
  other arithmetic  12.7 us (3%)
  matrix products  10.3 us (2%)
    psum x1, waiting for transfers between devices, body(): centroids = lax.psum(partial_sums, ('blk', 'col'))  270 us
    all_gather x1, waiting for transfers between devices, side_by_side(): lax.all_gather(both, axis, axis=dim, tiled=True)  63.7 us
    all_to_all x1, blocking collectives, sent_and_summed(): parts = lax.all_to_all(split_up(value, dim, peers), axis, 0, 0, tiled=True)  39.7 us
    gather x1, local copies, waits for them, and re-layouts, body(): live_cols = jnp.take(tile_mask, whole_rows // BLOCK, axis=1)  10.8 us
  transfers between devices with their start and end apart: 2, of which 2 were waited for; matrix products, arithmetic and copies ran while one was open for 4% of the time, Pallas kernels for 0%

commit v1 on v0

v1 whole, which is shorter than its diff:
```python
import math
import jax
import jax.numpy as jnp
from jax import lax
from jax.experimental import pallas as pl
from jax.experimental.pallas import tpu as pltpu
from jax.sharding import PartitionSpec as P

C = 1000
BLOCK = 128
MESH = pl.DeviceIdType.MESH
F32, BF16 = jnp.float32, jnp.bfloat16
NX, NY, NZ = 4, 8, 8
HALF = 64
DEAD = -1e30


def wrap(value, n):
    return lax.rem(value + n, n)


def device(x, y, core, z):
    x_high = lax.div(x, 2)
    x_low = x - 2 * x_high
    return {"blk": x_low * 16 + y * 2 + core, "col": x_high * 8 + z}


def rows_dot(a, b):
    return lax.dot_general(a, b, (((1,), (1,)), ((), ())), preferred_element_type=F32)


def split_rows_dot(ones, value, pieces):
    total, left = None, value
    for piece in range(pieces):
        part = left.astype(BF16)
        left = left - part.astype(F32)
        term = rows_dot(ones, part)
        total = term if total is None else total + term
    return total


def diagonal(row, n):
    square = jnp.broadcast_to(row, (n, n))
    down = lax.broadcasted_iota(jnp.int32, (n, n), 0)
    across = lax.broadcasted_iota(jnp.int32, (n, n), 1)
    return jnp.sum(jnp.where(down == across, square, 0.0), axis=1, keepdims=True)


class Sends:
    def __init__(self, sems):
        self.sems, self.used, self.open = sems, 0, []

    def start(self, src, dst, recv, to):
        copy = pltpu.make_async_remote_copy(
            src_ref=src, dst_ref=dst, send_sem=self.sems.at[self.used], recv_sem=recv,
            device_id=to, device_id_type=MESH,
        )
        self.used += 1
        copy.start()
        self.open.append(copy)

    def finish(self):
        for copy in self.open:
            copy.wait_send()


def arrived(ref, sems, index, frm):
    pltpu.make_async_remote_copy(
        src_ref=ref, dst_ref=ref, send_sem=sems.at[index], recv_sem=sems.at[index],
        device_id=frm, device_id_type=MESH,
    ).wait_recv()


def kernel(
    docs_ref, land_ref, vec_ref, ldeg_ref, eval_ref, mask_ref, label_ref,
    emb_ref, cent_ref,
    L, D, DC, M, KEEP, BIAS, PR, DG, PIN, DIN, SP, RP, SD, RD, G, SY, RY, RZ, W,
    local_sem, send_sem, y_sem, x_sem, core_sem, col_sem, cold_sem, g_sem, ry_sem, rz_sem, wy_sem, wx_sem, wc_sem,
):
    blk, col = lax.axis_index("blk"), lax.axis_index("col")
    x_low = lax.div(blk, 16)
    core = lax.rem(blk, 2)
    y = lax.rem(lax.div(blk, 2), 8)
    x_high = lax.div(col, 8)
    z = lax.rem(col, 8)
    x = x_high * 2 + x_low
    other = 1 - core
    features = docs_ref.shape[1]
    scale = 4.0 / features * math.log2(math.e)

    partner = device(x, y, other, z)
    up, down = device(x, wrap(y + 1, NY), core, z), device(x, wrap(y - 1, NY), core, z)
    right, left = device(wrap(x + 1, NX), y, core, z), device(wrap(x - 1, NX), y, core, z)

    own_docs = pltpu.make_async_copy(docs_ref, D.at[0], local_sem)
    own_docs.start()

    barrier = pltpu.get_barrier_semaphore()
    near = [partner]
    for d in range(1, NX):
        near += [device(wrap(x + d, NX), y, core, z), device(wrap(x + d, NX), y, other, z)]
    for d in range(1, NY):
        near.append(device(x, wrap(y + d, NY), core, z))
    for d in range(1, 16):
        near.append({"blk": blk, "col": lax.rem(col + d, 16)})
    near = near[:3] + near[4:]
    for peer in near:
        pl.semaphore_signal(barrier, inc=1, device_id=peer, device_id_type=MESH)

    inverse_root = diagonal(lax.rsqrt(ldeg_ref[...]), BLOCK)
    scaled = vec_ref[...].astype(F32) * inverse_root / eval_ref[...]
    L[y, 0:BLOCK, 0:features] = land_ref[...]
    L[y, 0:BLOCK, features:] = scaled.astype(BF16)
    M[0] = jnp.zeros(M.shape[1:], F32)
    M[0, 0:6, :] = mask_ref[...].astype(F32)
    pl.semaphore_wait(barrier, len(near))

    sends = Sends(send_sem)
    A, B = pl.ds(0, HALF), pl.ds(HALF, HALF)
    KINDS = {("A", 1): 0, ("B", 1): 1, ("A", -1): 2, ("B", -1): 3}

    def along_y(half, way, step):
        block = wrap(y - way * (step - 1), NY)
        piece = L.at[block, A if half == "A" else B]
        sends.start(piece, piece, y_sem.at[KINDS[half, way], step - 1], up if way == 1 else down)

    def along_x(half, offset):
        block = wrap(y + offset, NY)
        if half == "A":
            sends.start(L.at[block, A], L.at[block, pl.ds(2 * HALF, HALF)], x_sem.at[0, offset % NY], right)
        else:
            sends.start(L.at[block, B], L.at[block, pl.ds(3 * HALF, HALF)], x_sem.at[1, offset % NY], left)

    def from_y(half, way, step):
        block = wrap(y - way * step, NY)
        piece = L.at[block, A if half == "A" else B]
        arrived(piece, y_sem.at[KINDS[half, way]], step - 1, down if way == 1 else up)

    def from_x(offset):
        block = wrap(y + offset, NY)
        arrived(L.at[block, pl.ds(2 * HALF, HALF)], x_sem.at[0], offset % NY, left)
        arrived(L.at[block, pl.ds(3 * HALF, HALF)], x_sem.at[1], offset % NY, right)

    along_y("A", 1, 1)
    along_y("B", -1, 1)
    along_x("A", 0)
    along_x("B", 0)
    along_y("B", 1, 1)
    along_y("A", -1, 1)
    sends.start(M.at[0], M.at[1], core_sem.at[0], partner)
    own_docs.wait()
    sends.start(D.at[0], D.at[1], core_sem.at[1], partner)

    PR[...] = jnp.zeros(PR.shape, F32)
    DG[...] = jnp.zeros(DG.shape, F32)
    arrived(M.at[1], core_sem, 0, partner)
    live = M[...].reshape(16, M.shape[2])
    tiles = lax.broadcasted_iota(jnp.int32, live.shape, 1)
    segment = lax.div(lax.broadcasted_iota(jnp.int32, (16, 4 * HALF), 1), HALF)

    def tile_of(source_x, block):
        high = lax.div(source_x, 2)
        return (source_x - 2 * high) * 256 + block * 32 + core * 16 + high * 8 + z

    for block in range(NY):
        cols = [
            jnp.sum(jnp.where(tiles == tile_of(source, block), live, 0.0), axis=1, keepdims=True)
            for source in (x, wrap(x - 1, NX), wrap(x + 1, NX))
        ]
        keep = jnp.where(segment < 2, cols[0], jnp.where(segment < 3, cols[1], cols[2]))
        KEEP[block] = jnp.where(keep > 0.0, 0.0, DEAD)

    arrived(D.at[1], core_sem, 1, partner)

    def squares(chunk, carry):
        who, at = lax.div(chunk, 2), lax.rem(chunk, 2) * 384
        rows = D[who, pl.ds(pl.multiple_of(at, 384), 384), :].astype(F32)
        total = jnp.sum(rows * rows, axis=1, keepdims=True) * (-scale)
        DC[who, pl.ds(pl.multiple_of(at, 384), 384), :] = jnp.broadcast_to(total, (384, 128))
        return carry

    lax.fori_loop(0, 4, squares, 0)
    ones = jnp.ones((8, features), BF16)

    def prepare(offset):
        block = wrap(y + offset, NY)
        values = L[block, :, 0:features].astype(F32)
        norms = split_rows_dot(ones, values * values, 2)
        BIAS[...] = KEEP[block] - scale * norms[0:1, :]

    def multiply(offset, who, part):
        block = wrap(y + offset, NY)
        at = pl.multiple_of(part * 384, 384)
        docs = D[who, pl.ds(at, 384), :]
        products = rows_dot(docs, L[block, :, 0:features])
        shift = DC[who, pl.ds(at, 384), :]
        shift = jnp.concatenate([shift, shift], axis=1)
        bias = jnp.concatenate(
            [jnp.broadcast_to(BIAS[pl.ds(who * 8 + part * 3 + i, 1), :], (128, 256)) for i in range(3)], axis=0
        )
        weights = jnp.exp2(products * (2.0 * scale) + shift + bias)
        groups = pl.ds(part * 8, 8)
        DG[who, groups] += (weights[:, 0:128] + weights[:, 128:256]).reshape(8, 48, 128)
        total = jnp.dot(weights.astype(BF16), L[block, :, features:], preferred_element_type=F32)
        PR[who, groups] += total.reshape(8, 48, 256)

    def batch(offset):
        from_x(offset)
        prepare(offset)

        def part(index, carry):
            multiply(offset, 1 - lax.div(index, 2), lax.rem(index, 2))
            return carry

        lax.fori_loop(0, 4, part, 0)

    for step in range(1, 5):
        from_y("A", 1, step)
        if step < 4:
            along_y("A", 1, step + 1)
        along_x("A", -step)
        from_y("B", -1, step)
        if step < 4:
            along_y("B", -1, step + 1)
        along_x("B", step)
        batch(-(step - 1))
        if step < 4:
            from_y("B", 1, step)
            if step < 3:
                along_y("B", 1, step + 1)
            along_x("B", -step)
            from_y("A", -1, step)
            if step < 3:
                along_y("A", -1, step + 1)
            along_x("A", step)
        if step > 1:
            batch(step - 1)

    from_x(4)
    prepare(4)
    for who in (1, 0):
        def part(index, carry, who=who):
            multiply(4, who, index)
            return carry

        lax.fori_loop(0, 2, part, 0)
        if who == 1:
            sends.start(PR.at[1], PIN, core_sem.at[2], partner)
            sends.start(DG.at[1], DIN, core_sem.at[3], partner)

    arrived(PIN, core_sem, 2, partner)
    arrived(DIN, core_sem, 3, partner)
    ones = jnp.ones((8, 128), BF16)

    def degrees(at):
        return split_rows_dot(ones, DG[0, at] + DIN[at], 3)

    for d in range(1, 16):
        to = lax.rem(col + d, 16)
        owner = {"blk": blk, "col": to}
        SP[to] = (PR[0, to] + PIN[to]).astype(BF16)
        SD[to] = jnp.zeros((8, 128), F32)
        SD[to, :, 0:48] = degrees(to)
        sends.start(SP.at[to], RP.at[col], col_sem.at[d], owner)
        sends.start(SD.at[to], RD.at[col], cold_sem.at[d], owner)
    projection = PR[0, col] + PIN[col]
    degree = degrees(col)
    for d in range(1, 16):
        frm = lax.rem(col - d + 16, 16)
        owner = {"blk": blk, "col": frm}
        arrived(RP.at[frm], col_sem, d, owner)
        arrived(RD.at[frm], cold_sem, d, owner)
        projection = projection + RP[frm].astype(F32)
        degree = degree + RD[frm, :, 0:48]
    embedding = projection * lax.rsqrt(diagonal(degree[0:1, :], 48))
    emb_ref[...] = embedding
    unit = embedding * lax.rsqrt(jnp.sum(embedding * embedding, axis=1, keepdims=True) + 1e-6)

    mine = x * 2 + core
    label = label_ref[...]
    high = lax.div(label, 32)
    low = label - 32 * high
    two = lax.broadcasted_iota(jnp.int32, (16, 48), 0)
    coded = jnp.where(two == 0, jnp.broadcast_to(high, (16, 48)), jnp.broadcast_to(low, (16, 48)))
    G[mine, 0:48, :] = unit.astype(BF16)
    G[mine, 48:64, :] = jnp.zeros((16, 256), BF16)
    G[mine, 48:64, 0:48] = coded.astype(F32).astype(BF16)
    group = [(d, c) for d in range(NX) for c in range(2) if (d, c) != (0, 0)]
    for index, (d, c) in enumerate(group):
        other_core = core if c == 0 else other
        to = device(wrap(x + d, NX), y, other_core, z)
        sends.start(G.at[mine], G.at[mine], g_sem.at[index], to)
    for index, (d, c) in enumerate(group):
        other_core = core if c == 0 else other
        from_where = wrap(x - d, NX)
        slot = from_where * 2 + other_core
        arrived(G.at[slot], g_sem, index, device(from_where, y, other_core, z))
    clusters = (lax.broadcasted_iota(jnp.int32, (128, 48), 0) + mine * 128).astype(F32)
    sums = jnp.zeros((128, 256), F32)
    for source in range(8):
        code = G[source, 48:64, 0:48].astype(F32)
        which = code[0:1, :] * 32.0 + code[1:2, :]
        hot = jnp.where(clusters == which, 1.0, 0.0).astype(BF16)
        sums = sums + jnp.dot(hot, G[source, 0:48, :], preferred_element_type=F32)
    SY[...] = sums.reshape(8, 16, 256)

    for d in range(1, NY):
        to = wrap(y + d, NY)
        sends.start(SY.at[to], RY.at[y], ry_sem.at[d], device(x, to, core, z))
    RY[y] = SY[y]
    for d in range(1, NY):
        frm = wrap(y - d, NY)
        arrived(RY.at[frm], ry_sem, d, device(x, frm, core, z))
    total = RY[0]
    for source in range(1, NY):
        total = total + RY[source]
    RZ[z] = total

    for d in range(1, NZ):
        sends.start(RZ.at[z], RZ.at[z], rz_sem.at[d], device(x, y, core, wrap(z + d, NZ)))
    for d in range(1, NZ):
        frm = wrap(z - d, NZ)
        arrived(RZ.at[frm], rz_sem, d, device(x, y, core, frm))
    total = RZ[0]
    for source in range(1, NZ):
        total = total + RZ[source]
    W[mine, y] = total.astype(BF16)

    for d in range(1, NY):
        sends.start(W.at[mine, y], W.at[mine, y], wy_sem.at[d], device(x, wrap(y + d, NY), core, z))
    for d in range(1, NY):
        frm = wrap(y - d, NY)
        arrived(W.at[mine, frm], wy_sem, d, device(x, frm, core, z))
    for d in range(1, NX):
        sends.start(W.at[mine], W.at[mine], wx_sem.at[d], device(wrap(x + d, NX), y, core, z))
    sends.start(W.at[mine], W.at[mine], wc_sem.at[0], partner)
    for d in range(1, NX):
        frm = wrap(x - d, NX)
        slot = frm * 2 + core
        arrived(W.at[slot], wx_sem, d, device(frm, y, core, z))
        sends.start(W.at[slot], W.at[slot], wc_sem.at[d], partner)
    for d in range(NX):
        frm = wrap(x - d, NX)
        arrived(W.at[frm * 2 + other], wc_sem, d, partner)
    cent_ref[...] = W[...].reshape(1024, 256)
    sends.finish()


def body(documents, landmarks, eigen_vectors, land_degree, eigen_values, tile_mask, labels):
    rows, features = documents.shape
    k = eigen_vectors.shape[1]
    dma = pltpu.SemaphoreType.DMA
    vmem = pl.BlockSpec(memory_space=pltpu.VMEM)
    embedding, centroids = pl.pallas_call(
        kernel,
        out_shape=(jax.ShapeDtypeStruct((48, k), F32), jax.ShapeDtypeStruct((1024, k), BF16)),
        in_specs=[pl.BlockSpec(memory_space=pl.ANY)] + [vmem] * 6,
        out_specs=(vmem, vmem),
        scratch_shapes=[
            pltpu.VMEM((NY, 4 * HALF, features + k), BF16),
            pltpu.VMEM((2, rows, features), BF16),
            pltpu.VMEM((2, rows, 128), F32),
            pltpu.VMEM((2, 8, 512), F32),
            pltpu.VMEM((NY, 16, 4 * HALF), F32),
            pltpu.VMEM((16, 4 * HALF), F32),
            pltpu.VMEM((2, 16, 48, k), F32),
            pltpu.VMEM((2, 16, 48, 128), F32),
            pltpu.VMEM((16, 48, k), F32),
            pltpu.VMEM((16, 48, 128), F32),
            pltpu.VMEM((16, 48, k), BF16),
            pltpu.VMEM((16, 48, k), BF16),
            pltpu.VMEM((16, 8, 128), F32),
            pltpu.VMEM((16, 8, 128), F32),
            pltpu.VMEM((8, 64, k), BF16),
            pltpu.VMEM((8, 16, k), F32),
            pltpu.VMEM((8, 16, k), F32),
            pltpu.VMEM((8, 16, k), F32),
            pltpu.VMEM((8, 8, 16, k), BF16),
            dma(()),
            dma((128,)),
            dma((4, 4)),
            dma((2, 8)),
            dma((4,)),
            dma((16,)),
            dma((16,)),
            dma((8,)),
            dma((8,)),
            dma((8,)),
            dma((8,)),
            dma((4,)),
            dma((4,)),
        ],
        compiler_params=pltpu.CompilerParams(collective_id=0, has_side_effects=True),
        name="nystrom",
    )(
        documents, landmarks, eigen_vectors, land_degree[None, :], eigen_values[None, :], tile_mask, labels[None, :]
    )
    return embedding, centroids[:C].astype(F32)


def solution(mesh):
    placed = (
        P("blk", None),
        P(("blk", "col"), None),
        P(("blk", "col"), None),
        P(("blk", "col")),
        P(),
        P("blk", None),
        P(("blk", "col")),
    )
    return jax.shard_map(
        body, mesh=mesh, in_specs=placed, out_specs=(P(("blk", "col"), None), P()), check_vma=False
    )
```

time: 430 us -> 102 us (0.24)
  waiting for transfers between devices: 334 us -> 0 us
  Pallas kernels: 0 us -> 98.5 us
  blocking collectives: 39.7 us -> 0 us
  local copies, waits for them, and re-layouts: 17.9 us -> 0.62 us
  between operations: 14.8 us -> 0.65 us
  other arithmetic: 12.7 us -> 2.08 us
  matrix products: 10.3 us -> 0 us
    psum x1 -> x0, waiting for transfers between devices: 270 us -> none  [body(): centroids = lax.psum(partial_sums, ('blk', 'col'))]
    pallas_call x0 -> x1, Pallas kernels: none -> 98.5 us  [body(): pl.pallas_call(kernel, out_shape=(jax.ShapeDtypeStruct((48, k), F32), jax...]
    all_gather x1 -> x0, waiting for transfers between devices: 63.7 us -> none  [side_by_side(): lax.all_gather(both, axis, axis=dim, tiled=True)]
    all_to_all x1 -> x0, blocking collectives: 39.7 us -> none  [sent_and_summed(): parts = lax.all_to_all(split_up(value, dim, peers), axis, 0, 0, tiled=True)]
    gather x1 -> x0, local copies, waits for them, and re-layouts: 10.8 us -> none  [body(): live_cols = jnp.take(tile_mask, whole_rows // BLOCK, axis=1)]
    dot_general x3 -> x0, matrix products: 10.3 us -> none  [the longest x1 6.87 us: compute(): jnp.einsum('df,lf->dl', documents, land_piece, preferred_element_type=jnp...]
    reduce_sum x4 -> x0, other arithmetic: 4.86 us -> none  [the longest x1 4.38 us: compute(): land_square = jnp.sum(jnp.square(land_piece.astype(jnp.float32)), 1)]
  transfers between devices with their start and end apart: 2 -> 0, of which waited for: 2 -> 0; matrix products, arithmetic and copies ran while one was open for 4% -> 0% of each run, Pallas kernels for 0% -> 0%
where the time goes in v1:
time: 102 us
  Pallas kernels  98.5 us (97%)
  other arithmetic  2.08 us (2%)
    pallas_call x1, Pallas kernels, body(): pl.pallas_call(kernel, out_shape=(jax.ShapeDtypeStruct((48, k), F32), jax...  98.5 us
    convert_element_type x1, other arithmetic, body(): return (embedding, centroids[:C].astype(F32))  2.08 us

profile of v1, /device:TPU:1, one launch (start us, length us, event | category | flops | bytes accessed | tf_op | source)
XLA Modules:
  0.0 101.8 jit_solution(1610262185641763869)
XLA Ops:
  0.6 98.5 %nystrom.1 = (f32[48,256]{1,0:T(8,128)}, bf16[1024,256]{1,0:T(8,128)(2,1)}) custom-call(bf16[768,768]{1,0:T(8,128)(2,1)} %docs_ref.1, bf16[128,768]{1,0:T(8,128)(2,1)} %land_ref.1, bf16[128,256]{1,0:T(8,128)(2,1)} %vec_ref.1, f32[1,128]{1,0:T(1,128)} %bitcast.4, f32[1,256]{1,0:T(1,128)} %bitcast.3, s32[6,512]{1,0:T(8,128)} %mask_ref.1, s32[1,48]{1,0:T(1,128)} %bitcast.5), custom_call_target="tpu_custom_call" | custom-call | tf_op jit(solution)/shard_map/nystrom/pallas_call | solution.py:354
  99.1 0.0 copy-start
  99.1 2.1 %slice_convert_fusion = f32[1000,256]{1,0:T(8,128)} fusion(bf16[1024,256]{1,0:T(8,128)(2,1)} %get-tuple-element.5), kind=kLoop, calls=%fused_computation | loop fusion | flops 256000 | bytes 1536000 | tf_op jit(solution)/shard_map/convert_element_type | solution.py:398
  101.2 0.0 copy-done
  101.2 0.6 copy.10
Async XLA Ops:
  99.1 2.1 %copy-start = (f32[48,256]{1,0:T(8,128)S(1)}, f32[48,256]{1,0:T(8,128)}, u32[]{:S(2)}) copy-start(f32[48,256]{1,0:T(8,128)} %get-tuple-element.8) | copy-start | bytes 147460

commit v2 on v1

--- a/solution.py
+++ b/solution.py
@@ -74,8 +74,8 @@
 def kernel(
     docs_ref, land_ref, vec_ref, ldeg_ref, eval_ref, mask_ref, label_ref,
     emb_ref, cent_ref,
-    L, D, DC, M, KEEP, BIAS, PR, DG, PIN, DIN, SP, RP, SD, RD, G, SY, RY, RZ, W,
-    local_sem, send_sem, y_sem, x_sem, core_sem, col_sem, cold_sem, g_sem, ry_sem, rz_sem, wy_sem, wx_sem, wc_sem,
+    L, D, DC, M, KEEP, BIAS, PR, DG, PIN, DIN, SP, RP, SD, RD, LB, G, SY, RY, RZ, W,
+    local_sem, send_sem, y_sem, x_sem, core_sem, col_sem, cold_sem, g_sem, ry_sem, rz_sem, wy_sem, wx_sem, wc_sem, l_sem, word,
 ):
     blk, col = lax.axis_index("blk"), lax.axis_index("col")
     x_low = lax.div(blk, 16)
@@ -96,14 +96,8 @@
     own_docs.start()
 
     barrier = pltpu.get_barrier_semaphore()
-    near = [partner]
-    for d in range(1, NX):
-        near += [device(wrap(x + d, NX), y, core, z), device(wrap(x + d, NX), y, other, z)]
-    for d in range(1, NY):
-        near.append(device(x, wrap(y + d, NY), core, z))
-    for d in range(1, 16):
-        near.append({"blk": blk, "col": lax.rem(col + d, 16)})
-    near = near[:3] + near[4:]
+    front, back = device(x, y, core, wrap(z + 1, NZ)), device(x, y, core, wrap(z - 1, NZ))
+    near = [partner, up, down, right, left, front, back]
     for peer in near:
         pl.semaphore_signal(barrier, inc=1, device_id=peer, device_id_type=MESH)
 
@@ -190,7 +184,7 @@
 
     def multiply(offset, who, part):
         block = wrap(y + offset, NY)
-        at = pl.multiple_of(part * 384, 384)
+        at = part * 384 if isinstance(part, int) else pl.multiple_of(part * 384, 384)
         docs = D[who, pl.ds(at, 384), :]
         products = rows_dot(docs, L[block, :, 0:features])
         shift = DC[who, pl.ds(at, 384), :]
@@ -204,15 +198,32 @@
         total = jnp.dot(weights.astype(BF16), L[block, :, features:], preferred_element_type=F32)
         PR[who, groups] += total.reshape(8, 48, 256)
 
+    def multiply_all(offset, who):
+        block = wrap(y + offset, NY)
+        products = rows_dot(D[who], L[block, :, 0:features])
+        shift = jnp.concatenate([DC[who], DC[who]], axis=1)
+        bias = jnp.concatenate(
+            [jnp.broadcast_to(BIAS[who * 8 + i : who * 8 + i + 1, :], (128, 256)) for i in range(6)], axis=0
+        )
+        weights = jnp.exp2(products * (2.0 * scale) + shift + bias)
+        DG[who] += (weights[:, 0:128] + weights[:, 128:256]).reshape(16, 48, 128)
+        total = jnp.dot(weights.astype(BF16), L[block, :, features:], preferred_element_type=F32)
+        PR[who] += total.reshape(16, 48, 256)
+
     def batch(offset):
         from_x(offset)
         prepare(offset)
 
-        def part(index, carry):
-            multiply(offset, 1 - lax.div(index, 2), lax.rem(index, 2))
-            return carry
-
-        lax.fori_loop(0, 4, part, 0)
+        for who in (1, 0):
+            multiply_all(offset, who)
+
+    def tell(step):
+        pl.semaphore_signal(word.at[0, step], inc=1, device_id=front, device_id_type=MESH)
+        pl.semaphore_signal(word.at[1, step], inc=1, device_id=back, device_id_type=MESH)
+
+    def heard(step):
+        pl.semaphore_wait(word.at[0, step], 1)
+        pl.semaphore_wait(word.at[1, step], 1)
 
     for step in range(1, 5):
         from_y("A", 1, step)
@@ -224,6 +235,9 @@
             along_y("B", -1, step + 1)
         along_x("B", step)
         batch(-(step - 1))
+        if step > 1:
+            heard(step - 2)
+        tell(step - 1)
         if step < 4:
             from_y("B", 1, step)
             if step < 3:
@@ -236,45 +250,7 @@
         if step > 1:
             batch(step - 1)
 
-    from_x(4)
-    prepare(4)
-    for who in (1, 0):
-        def part(index, carry, who=who):
-            multiply(4, who, index)
-            return carry
-
-        lax.fori_loop(0, 2, part, 0)
-        if who == 1:
-            sends.start(PR.at[1], PIN, core_sem.at[2], partner)
-            sends.start(DG.at[1], DIN, core_sem.at[3], partner)
-
-    arrived(PIN, core_sem, 2, partner)
-    arrived(DIN, core_sem, 3, partner)
-    ones = jnp.ones((8, 128), BF16)
-
-    def degrees(at):
-        return split_rows_dot(ones, DG[0, at] + DIN[at], 3)
-
-    for d in range(1, 16):
-        to = lax.rem(col + d, 16)
-        owner = {"blk": blk, "col": to}
-        SP[to] = (PR[0, to] + PIN[to]).astype(BF16)
-        SD[to] = jnp.zeros((8, 128), F32)
-        SD[to, :, 0:48] = degrees(to)
-        sends.start(SP.at[to], RP.at[col], col_sem.at[d], owner)
-        sends.start(SD.at[to], RD.at[col], cold_sem.at[d], owner)
-    projection = PR[0, col] + PIN[col]
-    degree = degrees(col)
-    for d in range(1, 16):
-        frm = lax.rem(col - d + 16, 16)
-        owner = {"blk": blk, "col": frm}
-        arrived(RP.at[frm], col_sem, d, owner)
-        arrived(RD.at[frm], cold_sem, d, owner)
-        projection = projection + RP[frm].astype(F32)
-        degree = degree + RD[frm, :, 0:48]
-    embedding = projection * lax.rsqrt(diagonal(degree[0:1, :], 48))
-    emb_ref[...] = embedding
-    unit = embedding * lax.rsqrt(jnp.sum(embedding * embedding, axis=1, keepdims=True) + 1e-6)
+    heard(3)
 
     mine = x * 2 + core
     label = label_ref[...]
@@ -282,67 +258,125 @@
     low = label - 32 * high
     two = lax.broadcasted_iota(jnp.int32, (16, 48), 0)
     coded = jnp.where(two == 0, jnp.broadcast_to(high, (16, 48)), jnp.broadcast_to(low, (16, 48)))
-    G[mine, 0:48, :] = unit.astype(BF16)
-    G[mine, 48:64, :] = jnp.zeros((16, 256), BF16)
-    G[mine, 48:64, 0:48] = coded.astype(F32).astype(BF16)
+    LB[mine] = jnp.zeros((16, 128), BF16)
+    LB[mine, :, 0:48] = coded.astype(F32).astype(BF16)
     group = [(d, c) for d in range(NX) for c in range(2) if (d, c) != (0, 0)]
+
+    def member(d, c):
+        return wrap(x + d, NX), core if c == 0 else other
+
+    from_x(4)
+    prepare(4)
     for index, (d, c) in enumerate(group):
-        other_core = core if c == 0 else other
-        to = device(wrap(x + d, NX), y, other_core, z)
-        sends.start(G.at[mine], G.at[mine], g_sem.at[index], to)
+        to_x, to_core = member(d, c)
+        sends.start(LB.at[mine], LB.at[mine], l_sem.at[index], device(to_x, y, to_core, z))
+    far_first = (1 - x_high, x_high)
+    for turn, part in enumerate(far_first):
+        groups = pl.ds(part * 8, 8)
+        multiply(4, 1, part)
+        sends.start(PR.at[1, groups], PIN.at[groups], core_sem.at[2 + turn], partner)
+        sends.start(DG.at[1, groups], DIN.at[groups], core_sem.at[4 + turn], partner)
+    for part in far_first:
+        multiply(4, 0, part)
+
+    ones = jnp.ones((8, 128), BF16)
+
+    def degrees(at):
+        return split_rows_dot(ones, DG[0, at] + DIN[at], 3)[0:1, :]
+
+    for turn, part in enumerate(far_first):
+        groups = pl.ds(part * 8, 8)
+        arrived(PIN.at[groups], core_sem, 2 + turn, partner)
+        arrived(DIN.at[groups], core_sem, 4 + turn, partner)
+        for d in range(turn, NZ):
+            to = part * 8 + wrap(z + d, NZ)
+            owner = {"blk": blk, "col": to}
+            SP[to] = (PR[0, to] + PIN[to]).astype(BF16)
+            SD[to, :, 0:48] = degrees(to)
+            sends.start(SP.at[to], RP.at[col], col_sem.at[turn * 8 + d], owner)
+            sends.start(SD.at[to], RD.at[col], cold_sem.at[turn * 8 + d], owner)
+    projection = PR[0, col] + PIN[col]
+    degree = degrees(col)
+    for turn, part in enumerate(far_first):
+        for d in range(turn, NZ):
+            frm = part * 8 + wrap(z - d, NZ)
+            owner = {"blk": blk, "col": frm}
+            arrived(RP.at[frm], col_sem, turn * 8 + d, owner)
+            arrived(RD.at[frm], cold_sem, turn * 8 + d, owner)
+            projection = projection + RP[frm].astype(F32)
+            degree = degree + RD[frm, :, 0:48]
+    embedding = projection * lax.rsqrt(diagonal(degree, 48))
+    emb_ref[...] = embedding
+    unit = embedding * lax.rsqrt(jnp.sum(embedding * embedding, axis=1, keepdims=True) + 1e-6)
+
+    halves = (0,)
+    for h in halves:
+        G[h, mine] = unit.astype(BF16)
+        for index, (d, c) in enumerate(group):
+            to_x, to_core = member(d, c)
+            sends.start(G.at[h, mine], G.at[h, mine], g_sem.at[h, index], device(to_x, y, to_core, z))
     for index, (d, c) in enumerate(group):
-        other_core = core if c == 0 else other
-        from_where = wrap(x - d, NX)
-        slot = from_where * 2 + other_core
-        arrived(G.at[slot], g_sem, index, device(from_where, y, other_core, z))
+        frm_x, frm_core = member(-d, c)
+        arrived(LB.at[frm_x * 2 + frm_core], l_sem, index, device(frm_x, y, frm_core, z))
     clusters = (lax.broadcasted_iota(jnp.int32, (128, 48), 0) + mine * 128).astype(F32)
-    sums = jnp.zeros((128, 256), F32)
+    hot = []
     for source in range(8):
-        code = G[source, 48:64, 0:48].astype(F32)
+        code = LB[source, :, 0:48].astype(F32)
         which = code[0:1, :] * 32.0 + code[1:2, :]
-        hot = jnp.where(clusters == which, 1.0, 0.0).astype(BF16)
-        sums = sums + jnp.dot(hot, G[source, 0:48, :], preferred_element_type=F32)
-    SY[...] = sums.reshape(8, 16, 256)
-
-    for d in range(1, NY):
-        to = wrap(y + d, NY)
-        sends.start(SY.at[to], RY.at[y], ry_sem.at[d], device(x, to, core, z))
-    RY[y] = SY[y]
-    for d in range(1, NY):
-        frm = wrap(y - d, NY)
-        arrived(RY.at[frm], ry_sem, d, device(x, frm, core, z))
-    total = RY[0]
-    for source in range(1, NY):
-        total = total + RY[source]
-    RZ[z] = total
-
-    for d in range(1, NZ):
-        sends.start(RZ.at[z], RZ.at[z], rz_sem.at[d], device(x, y, core, wrap(z + d, NZ)))
-    for d in range(1, NZ):
-        frm = wrap(z - d, NZ)
-        arrived(RZ.at[frm], rz_sem, d, device(x, y, core, frm))
-    total = RZ[0]
-    for source in range(1, NZ):
-        total = total + RZ[source]
-    W[mine, y] = total.astype(BF16)
-
-    for d in range(1, NY):
-        sends.start(W.at[mine, y], W.at[mine, y], wy_sem.at[d], device(x, wrap(y + d, NY), core, z))
-    for d in range(1, NY):
-        frm = wrap(y - d, NY)
-        arrived(W.at[mine, frm], wy_sem, d, device(x, frm, core, z))
-    for d in range(1, NX):
-        sends.start(W.at[mine], W.at[mine], wx_sem.at[d], device(wrap(x + d, NX), y, core, z))
-    sends.start(W.at[mine], W.at[mine], wc_sem.at[0], partner)
-    for d in range(1, NX):
-        frm = wrap(x - d, NX)
-        slot = frm * 2 + core
-        arrived(W.at[slot], wx_sem, d, device(frm, y, core, z))
-        sends.start(W.at[slot], W.at[slot], wc_sem.at[d], partner)
-    for d in range(NX):
-        frm = wrap(x - d, NX)
-        arrived(W.at[frm * 2 + other], wc_sem, d, partner)
-    cent_ref[...] = W[...].reshape(1024, 256)
+        hot.append(jnp.where(clusters == which, 1.0, 0.0).astype(BF16))
+
+    for h in halves:
+        for index, (d, c) in enumerate(group):
+            frm_x, frm_core = member(-d, c)
+            arrived(G.at[h, frm_x * 2 + frm_core], g_sem.at[h], index, device(frm_x, y, frm_core, z))
+        sums = jnp.zeros((128, 256), F32)
+        for source in range(8):
+            sums = sums + jnp.dot(hot[source], G[h, source], preferred_element_type=F32)
+        SY[h] = sums.reshape(8, 16, 256)
+        for d in range(1, NY):
+            to = wrap(y + d, NY)
+            sends.start(SY.at[h, to], RY.at[h, y], ry_sem.at[h, d], device(x, to, core, z))
+
+    for h in halves:
+        RY[h, y] = SY[h, y]
+        for d in range(1, NY):
+            frm = wrap(y - d, NY)
+            arrived(RY.at[h, frm], ry_sem.at[h], d, device(x, frm, core, z))
+        total = RY[h, 0]
+        for source in range(1, NY):
+            total = total + RY[h, source]
+        RZ[h, z] = total
+        for d in range(1, NZ):
+            sends.start(RZ.at[h, z], RZ.at[h, z], rz_sem.at[h, d], device(x, y, core, wrap(z + d, NZ)))
+
+    for h in halves:
+        for d in range(1, NZ):
+            frm = wrap(z - d, NZ)
+            arrived(RZ.at[h, frm], rz_sem.at[h], d, device(x, y, core, frm))
+        total = RZ[h, 0]
+        for source in range(1, NZ):
+            total = total + RZ[h, source]
+        W[h, mine, y] = total.astype(BF16)
+        for d in range(1, NY):
+            sends.start(W.at[h, mine, y], W.at[h, mine, y], wy_sem.at[h, d], device(x, wrap(y + d, NY), core, z))
+    for h in halves:
+        for d in range(1, NY):
+            frm = wrap(y - d, NY)
+            arrived(W.at[h, mine, frm], wy_sem.at[h], d, device(x, frm, core, z))
+        for d in range(1, NX):
+            sends.start(W.at[h, mine], W.at[h, mine], wx_sem.at[h, d], device(wrap(x + d, NX), y, core, z))
+        sends.start(W.at[h, mine], W.at[h, mine], wc_sem.at[h, 0], partner)
+    for h in halves:
+        for d in range(1, NX):
+            frm = wrap(x - d, NX)
+            slot = frm * 2 + core
+            arrived(W.at[h, slot], wx_sem.at[h], d, device(frm, y, core, z))
+            sends.start(W.at[h, slot], W.at[h, slot], wc_sem.at[h, d], partner)
+    for h in halves:
+        for d in range(NX):
+            frm = wrap(x - d, NX)
+            arrived(W.at[h, frm * 2 + other], wc_sem.at[h], d, partner)
+        cent_ref[...] = W[h].reshape(1024, 256)
     sends.finish()
 
 
@@ -369,26 +403,29 @@
             pltpu.VMEM((16, 48, 128), F32),
             pltpu.VMEM((16, 48, k), BF16),
             pltpu.VMEM((16, 48, k), BF16),
-            pltpu.VMEM((16, 8, 128), F32),
-            pltpu.VMEM((16, 8, 128), F32),
-            pltpu.VMEM((8, 64, k), BF16),
-            pltpu.VMEM((8, 16, k), F32),
-            pltpu.VMEM((8, 16, k), F32),
-            pltpu.VMEM((8, 16, k), F32),
-            pltpu.VMEM((8, 8, 16, k), BF16),
+            pltpu.VMEM((16, 1, 128), F32),
+            pltpu.VMEM((16, 1, 128), F32),
+            pltpu.VMEM((8, 16, 128), BF16),
+            pltpu.VMEM((1, 8, 48, 256), BF16),
+            pltpu.VMEM((1, 8, 16, 256), F32),
+            pltpu.VMEM((1, 8, 16, 256), F32),
+            pltpu.VMEM((1, 8, 16, 256), F32),
+            pltpu.VMEM((1, 8, 8, 16, 256), BF16),
             dma(()),
-            dma((128,)),
+            dma((192,)),
             dma((4, 4)),
             dma((2, 8)),
-            dma((4,)),
+            dma((8,)),
             dma((16,)),
             dma((16,)),
+            dma((1, 8)),
+            dma((1, 8)),
+            dma((1, 8)),
+            dma((1, 8)),
+            dma((1, 4)),
+            dma((1, 4)),
             dma((8,)),
-            dma((8,)),
-            dma((8,)),
-            dma((8,)),
-            dma((4,)),
-            dma((4,)),
+            pltpu.SemaphoreType.REGULAR((2, 4)),
         ],
         compiler_params=pltpu.CompilerParams(collective_id=0, has_side_effects=True),
         name="nystrom",

time: 102 us -> 92.3 us (0.905)
  Pallas kernels: 98.5 us -> 88.8 us
    pallas_call x1, Pallas kernels: 98.5 us -> 88.8 us  [body(): pl.pallas_call(kernel, out_shape=(jax.ShapeDtypeStruct((48, k), F32), jax...]
where the time goes in v2:
time: 92.3 us; the launch traced here: 92.1 us
  Pallas kernels  88.8 us (96%)
  other arithmetic  2.08 us (2%)
    pallas_call x1, Pallas kernels, body(): pl.pallas_call(kernel, out_shape=(jax.ShapeDtypeStruct((48, k), F32), jax...  88.8 us
    convert_element_type x1, other arithmetic, body(): return (embedding, centroids[:C].astype(F32))  2.08 us

profile of v2, /device:TPU:1, one launch (start us, length us, event | category | flops | bytes accessed | tf_op | source)
XLA Modules:
  0.0 92.1 jit_solution(3538007215938125397)
XLA Ops:
  0.6 88.8 %nystrom.1 = (f32[48,256]{1,0:T(8,128)}, bf16[1024,256]{1,0:T(8,128)(2,1)}) custom-call(bf16[768,768]{1,0:T(8,128)(2,1)} %docs_ref.1, bf16[128,768]{1,0:T(8,128)(2,1)} %land_ref.1, bf16[128,256]{1,0:T(8,128)(2,1)} %vec_ref.1, f32[1,128]{1,0:T(1,128)} %bitcast.4, f32[1,256]{1,0:T(1,128)} %bitcast.3, s32[6,512]{1,0:T(8,128)} %mask_ref.1, s32[1,48]{1,0:T(1,128)} %bitcast.5), custom_call_target="tpu_custom_call" | custom-call | tf_op jit(solution)/shard_map/nystrom/pallas_call | solution.py:388
  89.4 0.0 copy-start
  89.4 2.1 %slice_convert_fusion = f32[1000,256]{1,0:T(8,128)} fusion(bf16[1024,256]{1,0:T(8,128)(2,1)} %get-tuple-element.5), kind=kLoop, calls=%fused_computation | loop fusion | flops 256000 | bytes 1536000 | tf_op jit(solution)/shard_map/convert_element_type | solution.py:435
  91.5 0.0 copy-done
  91.5 0.6 copy.10
Async XLA Ops:
  89.4 2.1 %copy-start = (f32[48,256]{1,0:T(8,128)S(1)}, f32[48,256]{1,0:T(8,128)}, u32[]{:S(2)}) copy-start(f32[48,256]{1,0:T(8,128)} %get-tuple-element.8) | copy-start | bytes 147460

commit v3 on v2

--- a/solution.py
+++ b/solution.py
@@ -11,6 +11,7 @@
 MESH = pl.DeviceIdType.MESH
 F32, BF16 = jnp.float32, jnp.bfloat16
 NX, NY, NZ = 4, 8, 8
+FAR_FIRST = (4, 3, 5, 2, 6, 1, 7)
 HALF = 64
 DEAD = -1e30
 
@@ -75,7 +76,7 @@
     docs_ref, land_ref, vec_ref, ldeg_ref, eval_ref, mask_ref, label_ref,
     emb_ref, cent_ref,
     L, D, DC, M, KEEP, BIAS, PR, DG, PIN, DIN, SP, RP, SD, RD, LB, G, SY, RY, RZ, W,
-    local_sem, send_sem, y_sem, x_sem, core_sem, col_sem, cold_sem, g_sem, ry_sem, rz_sem, wy_sem, wx_sem, wc_sem, l_sem, word,
+    local_sem, send_sem, y_sem, x_sem, core_sem, col_sem, cold_sem, g_sem, ry_sem, rz_sem, wy_sem, wx_sem, wc_sem, l_sem, word, last_sem,
 ):
     blk, col = lax.axis_index("blk"), lax.axis_index("col")
     x_low = lax.div(blk, 16)
@@ -225,15 +226,44 @@
         pl.semaphore_wait(word.at[0, step], 1)
         pl.semaphore_wait(word.at[1, step], 1)
 
+    last = wrap(y + 4, NY)
+    nearly = wrap(y - 3, NY), wrap(y + 3, NY)
+
+    def last_along_y():
+        for piece in (0, 1):
+            a = L.at[nearly[0], pl.ds(piece * 32, 32)]
+            sends.start(a, a, last_sem.at[0, piece], up)
+            b = L.at[nearly[1], pl.ds(HALF + piece * 32, 32)]
+            sends.start(b, b, last_sem.at[1, piece], down)
+
+    def last_along_x():
+        for piece in (0, 1):
+            a = L.at[last, pl.ds(piece * 32, 32)]
+            arrived(a, last_sem.at[0], piece, down)
+            sends.start(a, L.at[last, pl.ds(2 * HALF + piece * 32, 32)], last_sem.at[2, piece], right)
+            b = L.at[last, pl.ds(HALF + piece * 32, 32)]
+            arrived(b, last_sem.at[1], piece, up)
+            sends.start(b, L.at[last, pl.ds(3 * HALF + piece * 32, 32)], last_sem.at[3, piece], left)
+
+    def last_from_x():
+        for piece in (0, 1):
+            arrived(L.at[last, pl.ds(2 * HALF + piece * 32, 32)], last_sem.at[2], piece, left)
+            arrived(L.at[last, pl.ds(3 * HALF + piece * 32, 32)], last_sem.at[3], piece, right)
+
     for step in range(1, 5):
-        from_y("A", 1, step)
-        if step < 4:
-            along_y("A", 1, step + 1)
-        along_x("A", -step)
-        from_y("B", -1, step)
-        if step < 4:
-            along_y("B", -1, step + 1)
-        along_x("B", step)
+        if step == 4:
+            last_along_x()
+        else:
+            from_y("A", 1, step)
+            if step < 3:
+                along_y("A", 1, step + 1)
+            along_x("A", -step)
+            from_y("B", -1, step)
+            if step < 3:
+                along_y("B", -1, step + 1)
+            else:
+                last_along_y()
+            along_x("B", step)
         batch(-(step - 1))
         if step > 1:
             heard(step - 2)
@@ -265,7 +295,7 @@
     def member(d, c):
         return wrap(x + d, NX), core if c == 0 else other
 
-    from_x(4)
+    last_from_x()
     prepare(4)
     for index, (d, c) in enumerate(group):
         to_x, to_core = member(d, c)
@@ -288,7 +318,7 @@
         groups = pl.ds(part * 8, 8)
         arrived(PIN.at[groups], core_sem, 2 + turn, partner)
         arrived(DIN.at[groups], core_sem, 4 + turn, partner)
-        for d in range(turn, NZ):
+        for d in FAR_FIRST + (0,) * (1 - turn):
             to = part * 8 + wrap(z + d, NZ)
             owner = {"blk": blk, "col": to}
             SP[to] = (PR[0, to] + PIN[to]).astype(BF16)
@@ -332,8 +362,8 @@
         sums = jnp.zeros((128, 256), F32)
         for source in range(8):
             sums = sums + jnp.dot(hot[source], G[h, source], preferred_element_type=F32)
-        SY[h] = sums.reshape(8, 16, 256)
-        for d in range(1, NY):
+        SY[h] = sums.reshape(8, 16, 256).astype(BF16)
+        for d in FAR_FIRST:
             to = wrap(y + d, NY)
             sends.start(SY.at[h, to], RY.at[h, y], ry_sem.at[h, d], device(x, to, core, z))
 
@@ -342,22 +372,22 @@
         for d in range(1, NY):
             frm = wrap(y - d, NY)
             arrived(RY.at[h, frm], ry_sem.at[h], d, device(x, frm, core, z))
-        total = RY[h, 0]
+        total = RY[h, 0].astype(F32)
         for source in range(1, NY):
-            total = total + RY[h, source]
-        RZ[h, z] = total
-        for d in range(1, NZ):
+            total = total + RY[h, source].astype(F32)
+        RZ[h, z] = total.astype(BF16)
+        for d in FAR_FIRST:
             sends.start(RZ.at[h, z], RZ.at[h, z], rz_sem.at[h, d], device(x, y, core, wrap(z + d, NZ)))
 
     for h in halves:
         for d in range(1, NZ):
             frm = wrap(z - d, NZ)
             arrived(RZ.at[h, frm], rz_sem.at[h], d, device(x, y, core, frm))
-        total = RZ[h, 0]
+        total = RZ[h, 0].astype(F32)
         for source in range(1, NZ):
-            total = total + RZ[h, source]
+            total = total + RZ[h, source].astype(F32)
         W[h, mine, y] = total.astype(BF16)
-        for d in range(1, NY):
+        for d in FAR_FIRST:
             sends.start(W.at[h, mine, y], W.at[h, mine, y], wy_sem.at[h, d], device(x, wrap(y + d, NY), core, z))
     for h in halves:
         for d in range(1, NY):
@@ -407,9 +437,9 @@
             pltpu.VMEM((16, 1, 128), F32),
             pltpu.VMEM((8, 16, 128), BF16),
             pltpu.VMEM((1, 8, 48, 256), BF16),
-            pltpu.VMEM((1, 8, 16, 256), F32),
-            pltpu.VMEM((1, 8, 16, 256), F32),
-            pltpu.VMEM((1, 8, 16, 256), F32),
+            pltpu.VMEM((1, 8, 16, 256), BF16),
+            pltpu.VMEM((1, 8, 16, 256), BF16),
+            pltpu.VMEM((1, 8, 16, 256), BF16),
             pltpu.VMEM((1, 8, 8, 16, 256), BF16),
             dma(()),
             dma((192,)),
@@ -426,6 +456,7 @@
             dma((1, 4)),
             dma((8,)),
             pltpu.SemaphoreType.REGULAR((2, 4)),
+            dma((4, 2)),
         ],
         compiler_params=pltpu.CompilerParams(collective_id=0, has_side_effects=True),
         name="nystrom",

time: 92.3 us -> 89.2 us (0.966)
  Pallas kernels: 88.8 us -> 85.7 us
    pallas_call x1, Pallas kernels: 88.8 us -> 85.7 us  [body(): pl.pallas_call(kernel, out_shape=(jax.ShapeDtypeStruct((48, k), F32), jax...]
where the time goes in v3:
time: 89.2 us; the launch traced here: 89.1 us
  Pallas kernels  85.7 us (96%)
  other arithmetic  2.08 us (2%)
    pallas_call x1, Pallas kernels, body(): pl.pallas_call(kernel, out_shape=(jax.ShapeDtypeStruct((48, k), F32), jax...  85.7 us
    convert_element_type x1, other arithmetic, body(): return (embedding, centroids[:C].astype(F32))  2.08 us

profile of v3, /device:TPU:1, one launch (start us, length us, event | category | flops | bytes accessed | tf_op | source)
XLA Modules:
  0.0 89.1 jit_solution(11687142783428608776)
XLA Ops:
  0.6 85.7 %nystrom.1 = (f32[48,256]{1,0:T(8,128)}, bf16[1024,256]{1,0:T(8,128)(2,1)}) custom-call(bf16[768,768]{1,0:T(8,128)(2,1)} %docs_ref.1, bf16[128,768]{1,0:T(8,128)(2,1)} %land_ref.1, bf16[128,256]{1,0:T(8,128)(2,1)} %vec_ref.1, f32[1,128]{1,0:T(1,128)} %bitcast.4, f32[1,256]{1,0:T(1,128)} %bitcast.3, s32[6,512]{1,0:T(8,128)} %mask_ref.1, s32[1,48]{1,0:T(1,128)} %bitcast.5), custom_call_target="tpu_custom_call" | custom-call | tf_op jit(solution)/shard_map/nystrom/pallas_call | solution.py:418
  86.4 0.0 copy-start
  86.4 2.1 %slice_convert_fusion = f32[1000,256]{1,0:T(8,128)} fusion(bf16[1024,256]{1,0:T(8,128)(2,1)} %get-tuple-element.5), kind=kLoop, calls=%fused_computation | loop fusion | flops 256000 | bytes 1536000 | tf_op jit(solution)/shard_map/convert_element_type | solution.py:466
  88.5 0.0 copy-done
  88.5 0.6 copy.10
Async XLA Ops:
  86.4 2.1 %copy-start = (f32[48,256]{1,0:T(8,128)S(1)}, f32[48,256]{1,0:T(8,128)}, u32[]{:S(2)}) copy-start(f32[48,256]{1,0:T(8,128)} %get-tuple-element.8) | copy-start | bytes 147460
